TPU v7x, 32 devices: a whole 2x2x4 slice. The times are simulated.
32 devices in a mesh: dp: 8 (over y, x, core), tensor: 4 (over z).
Axes of the slice: x: 2, y: 2, z: 4, core: 2. Of those that a mesh axis runs over, the one named last changes fastest.
Arguments:
- grad_tokens: bfloat16 [1536, 2048], P('dp', 'tensor'), may hold values from -6 to 6
- hidden_input: bfloat16 [2048, 5120], P('dp', 'tensor'), may hold values from -6 to 6
- output_weight: bfloat16 [5120, 2048], P(None, 'tensor'), may hold values from -0.078125 to 0.078125
- image_tokens: int32 [8, 8], replicated, may hold values from 0 to 192, as said below
- moved_images: int32 [8], replicated, may hold values from 0 to 7, as said below
Outputs:
- input_grad: bfloat16 [2048, 5120], P('dp', 'tensor')
- weight_grad: float32 [5120, 2048], P('dp', 'tensor')
- bias_grad: float32 [2048], P('tensor')
Inputs may be any that keep to these rules, and one draw needn't show every extreme that they name: `image_tokens`: row s lists the merged tokens of sample s's images in order: 1 to 8 positive entries, then zeros; each row sums to 192. `moved_images`: entry s is less than the number of images of sample s; those trailing images hold at most 64 merged tokens together, exactly 64 for some sample in every draw. They are encoded by owner s + 1 (owner 0 after the last).
All inputs are finite; a program needn't handle non-finite values.
Results may differ from a plain program's by a relative error of at most 0.014.
Values may be sent and summed in bfloat16 or wider, within the bound.
A program may use at most 64 MiB of HBM per device.

v0:
```python
import functools

import jax
import jax.numpy as jnp
from jax import lax
from jax.experimental import pallas as pl
from jax.experimental.pallas import tpu as pltpu
from jax.sharding import PartitionSpec as P

root_half = 0.7071067811865476
inv_root_tau = 0.3989422804014327
MESH = pl.DeviceIdType.MESH
F32 = jnp.float32
BF16 = jnp.bfloat16


def from_behind(value, axis, steps):
    count = lax.axis_size(axis)
    pairs = [(source, (source + steps) % count) for source in range(count)]
    return lax.ppermute(value, axis, pairs)


def gelu_parts(values):
    normal_cdf = 0.5 * (1.0 + lax.erf(values * root_half))
    density = jnp.exp(-0.5 * values * values) * inv_root_tau
    return (values * normal_cdf, normal_cdf + values * density)


def kept_lengths(image_tokens, moved_images):
    present = jnp.sum((image_tokens > 0).astype(jnp.int32), axis=1)
    slot_ids = jnp.arange(image_tokens.shape[1], dtype=jnp.int32)
    kept_mask = slot_ids[None, :] < (present - moved_images)[:, None]
    return jnp.sum(jnp.where(kept_mask, image_tokens, 0), axis=1)


def per_device_any(grad_tokens, hidden_input, output_weight, image_tokens, moved_images):
    dp_count = lax.axis_size("dp")
    dp_index = lax.axis_index("dp")
    tok_rows = grad_tokens.shape[0]
    buffer_rows = hidden_input.shape[0]
    tail_count = buffer_rows - tok_rows
    keep_len = kept_lengths(image_tokens, moved_images)
    own_keep = jnp.sum(jnp.where(jnp.arange(dp_count, dtype=jnp.int32) == dp_index, keep_len, 0))
    positions = jnp.arange(tok_rows, dtype=jnp.int32)[:, None]
    zero_value = jnp.zeros((), BF16)
    kept_rows = jnp.where(positions < own_keep, grad_tokens, zero_value)
    moving = jnp.where(
        positions[tok_rows - tail_count :] >= own_keep,
        grad_tokens[tok_rows - tail_count :],
        zero_value,
    )
    arrived = from_behind(moving, "dp", 1)
    grad_rows = jnp.concatenate([kept_rows, arrived], axis=0)
    bias_grad = lax.psum(jnp.sum(grad_tokens.astype(F32), axis=0), "dp")
    activation, slopes = gelu_parts(hidden_input.astype(F32))
    partials = lax.dot_general(
        grad_rows, output_weight, (((1,), (1,)), ((), ())), preferred_element_type=F32
    )
    grad_hidden = lax.psum_scatter(
        partials.astype(BF16), "tensor", scatter_dimension=1, tiled=True
    ).astype(F32)
    input_grad = (grad_hidden * slopes).astype(BF16)
    full_act = lax.all_gather(activation.astype(BF16), "tensor", axis=1, tiled=True)
    hidden_width = full_act.shape[1]
    rows_each = (hidden_width + 8 * dp_count - 1) // (8 * dp_count) * 8
    padded = jnp.pad(full_act, ((0, 0), (0, rows_each * dp_count - hidden_width)))
    weight_grad = lax.psum_scatter(
        lax.dot_general(
            padded, grad_rows, (((0,), (0,)), ((), ())), preferred_element_type=F32
        ),
        "dp",
        scatter_dimension=0,
        tiled=True,
    )
    return (input_grad, weight_grad, bias_grad)


def kernel(
    n, dpn,
    g_ref, x_ref, w_hbm, it_ref, mv_ref,
    xg_ref, wg_ref, bg_ref,
    w_ref, raw, tail, act, act_other, slope, grad, part, sbuf, up_in, dn_in, wsend, wrecv, wmid, bias,
    w_sem, core_s, core_r, act_s, act_r, tail_s, tail_r,
    up_s, up_r, dn_s, dn_r, pl_s, pl_r, mid_r, bi_s, bi_r,
):
    dp = lax.axis_index("dp")
    z = lax.axis_index("tensor")
    core = lax.rem(dp, 2)
    chip = lax.div(dp, 2)
    partner = dp + 1 - 2 * core
    chips = dpn // 2
    tok = g_ref.shape[0]
    rows = x_ref.shape[0]
    width = x_ref.shape[1]
    half = width // 2
    tails = rows - tok

    wcopy = pltpu.make_async_copy(w_hbm, w_ref, w_sem)
    wcopy.start()

    barrier = pltpu.get_barrier_semaphore()
    for k in range(1, dpn):
        pl.semaphore_signal(barrier, inc=1, device_id=(lax.rem(dp + k, dpn), z), device_id_type=MESH)

    @pl.when(z > 0)
    def _():
        pl.semaphore_signal(barrier, inc=1, device_id=(dp, z - 1), device_id_type=MESH)

    @pl.when(z < n - 1)
    def _():
        pl.semaphore_signal(barrier, inc=1, device_id=(dp, z + 1), device_id_type=MESH)

    pl.semaphore_wait(barrier, dpn - 1 + jnp.where(z > 0, 1, 0) + jnp.where(z < n - 1, 1, 0))

    def remote(src, dst, ss, rs, d, t):
        return pltpu.make_async_remote_copy(
            src_ref=src, dst_ref=dst, send_sem=ss, recv_sem=rs, device_id=(d, t), device_id_type=MESH
        )

    lane = 128
    nk = half // lane
    ptile = width // nk

    raw_copy = remote(g_ref, raw, core_s, core_r, partner, z)
    tail_src = g_ref.at[pl.ds(tok - tails, tails)]
    tail_copies = [
        remote(tail_src, tail, tail_s.at[k], tail_r, lax.rem(dp + 1 + k, dpn), z) for k in range(2)
    ]

    def act_copy(k):
        return remote(act_other.at[k], act.at[z, k, core], act_s.at[k], act_r.at[k], partner, z)

    step_rows = 64

    def gelu_tile(which, k, to_other):
        cols = pl.ds(pl.multiple_of(which * half + k * lane, lane), lane)

        def body(i, carry):
            rs = pl.ds(pl.multiple_of(i * step_rows, step_rows), step_rows)
            a, s = gelu_parts(x_ref[rs, cols].astype(F32))
            slope[rs, cols] = s
            if to_other:
                act_other[k, rs, :] = a.astype(BF16)
            else:
                act[z, k, core, rs, :] = a.astype(BF16)
            return carry

        lax.fori_loop(0, rows // step_rows, body, 0)

    def up_ag(h, k, r):
        return remote(act.at[h, k], act.at[h, k], up_s.at[r, k], up_r.at[r, k], dp, z + 1)

    def dn_ag(h, k, r):
        return remote(act.at[h, k], act.at[h, k], dn_s.at[r, k], dn_r.at[r, k], dp, z - 1)

    def up_rs(h, k, r):
        return remote(sbuf.at[h, k], up_in.at[h, k], up_s.at[r, k], up_r.at[r, k], dp, z + 1)

    def dn_rs(h, k, r):
        return remote(sbuf.at[h, k], dn_in.at[h, k], dn_s.at[r, k], dn_r.at[r, k], dp, z - 1)

    def send_own(k):
        act_copy(k).wait_recv()

        @pl.when(z < n - 1)
        def _():
            up_ag(z, k, 0).start()

        @pl.when(z > 0)
        def _():
            dn_ag(z, k, 0).start()

    for k in range(nk):
        gelu_tile(1 - core, k, True)
        act_copy(k).start()
        if k == 0:
            raw_copy.start()

            @pl.when(core == 1)
            def _():
                for c in tail_copies:
                    c.start()

        gelu_tile(core, k, False)
        if k > 0:
            send_own(k - 1)
    send_own(nk - 1)

    raw_copy.wait_recv()
    chip_sum = jnp.sum(g_ref[...].astype(F32), axis=0, keepdims=True) + jnp.sum(
        raw[...].astype(F32), axis=0, keepdims=True
    )
    bias[chip] = jnp.broadcast_to(chip_sum, bias.shape[1:])

    def keep_of(s):
        images = it_ref[pl.ds(s, 1), :].astype(F32)
        present = jnp.sum(jnp.where(images > 0, 1.0, 0.0), axis=1, keepdims=True)
        ids = lax.broadcasted_iota(jnp.int32, images.shape, 1).astype(F32)
        kept = jnp.where(ids < present - mv_ref[s].astype(F32), images, 0.0)
        return jnp.sum(kept, axis=1, keepdims=True)

    place = lax.broadcasted_iota(jnp.int32, (tok, g_ref.shape[1]), 0).astype(F32)
    zero = jnp.zeros((), F32)

    def masked_own(block, s):
        return jnp.where(place < keep_of(s), block.astype(F32), zero).astype(BF16)

    def masked_tail(block, s):
        return jnp.where(place[tok - tails :] >= keep_of(s), block.astype(F32), zero).astype(BF16)

    grad[core, 0:tok, :] = masked_own(g_ref[...], dp)
    grad[1 - core, 0:tok, :] = masked_own(raw[...], partner)
    first = 2 * chip

    @pl.when(core == 0)
    def _():
        grad[1, tok:rows, :] = masked_tail(g_ref[pl.ds(tok - tails, tails), :], first)

    @pl.when(core == 1)
    def _():
        grad[1, tok:rows, :] = masked_tail(raw[pl.ds(tok - tails, tails), :], first)

    tail_copies[0].wait_recv()
    grad[0, tok:rows, :] = masked_tail(tail[...], lax.rem(first + dpn - 1, dpn))

    def bias_copy(k):
        return remote(
            bias.at[chip], bias.at[chip], bi_s.at[k], bi_r.at[chip], lax.rem(dp + 2 * k, dpn), z
        )

    for k in range(1, chips):
        bias_copy(k).start()

    wcopy.wait()

    def all_h(i, carry):
        h = lax.div(i, nk)
        k = lax.rem(i, nk)
        at = pl.ds(pl.multiple_of(i * ptile, ptile), ptile)
        part[h, k] = lax.dot_general(
            grad[core], w_ref[at, :], (((1,), (1,)), ((), ())), preferred_element_type=F32
        )
        return carry

    lax.fori_loop(0, n * nk, all_h, 0)

    @pl.when(z == 0)
    def _():
        for r in range(1, n):
            for k in range(nk):
                sbuf[n - r, k] = part[n - r, k].astype(BF16)
                up_rs(n - r, k, r).start()

    @pl.when(z == n - 1)
    def _():
        for r in range(1, n):
            for k in range(nk):
                sbuf[r - 1, k] = part[r - 1, k].astype(BF16)
                dn_rs(r - 1, k, r).start()

    piece = lane // 2

    def relation(h):
        return jnp.where(lax.rem(chip, 2) != lax.rem(h, 2), 1, 0) + jnp.where(
            lax.div(chip, 2) != lax.div(h, 2), 2, 0
        )

    along_x = chip + 1 - 2 * lax.rem(chip, 2)
    along_y = lax.rem(chip + 2, chips)

    def owner_copy(h, k, j):
        role = relation(h) - 1
        return remote(
            wsend.at[h, k, j], wrecv.at[role, k, j], pl_s.at[h, k, j], pl_r.at[role, k, j], h * 2 + core, z
        )

    def corner_copy(h, k, j):
        through = along_x if j == 0 else along_y
        return remote(
            wsend.at[h, k, j], wmid.at[1 - j, k], pl_s.at[h, k, j], mid_r.at[1 - j, k], through * 2 + core, z
        )

    def merge(h, k):
        rel = relation(h)
        for role in (1, 2):
            late = 1 if role == 1 else 0

            @pl.when(rel == role)
            def _():
                corner_copy(h, k, late).wait_recv()
                wsend[h, k, late] = (
                    wsend[h, k, late].astype(F32) + wmid[role - 1, k].astype(F32)
                ).astype(BF16)
                owner_copy(h, k, late).start()

    def weight_tile(h, k):
        acc = lax.dot_general(
            act[h, k, 0], grad[0], (((0,), (0,)), ((), ())), preferred_element_type=F32
        ) + lax.dot_general(
            act[h, k, 1], grad[1], (((0,), (0,)), ((), ())), preferred_element_type=F32
        )
        rel = relation(h)

        @pl.when(rel == 0)
        def _():
            wg_ref[k * lane : (k + 1) * lane, :] = acc

        @pl.when(rel != 0)
        def _():
            for j in range(2):
                wsend[h, k, j] = acc[j * piece : (j + 1) * piece].astype(BF16)

        @pl.when(rel == 1)
        def _():
            owner_copy(h, k, 0).start()

        @pl.when(rel == 2)
        def _():
            owner_copy(h, k, 1).start()

        @pl.when(rel == 3)
        def _():
            for j in range(2):
                corner_copy(h, k, j).start()

    for k in range(nk):
        weight_tile(z, k)

    def merge_round(r, k):
        if r == 0:
            merge(z, k)
        else:

            @pl.when(z >= r)
            def _():
                merge(z - r, k)

            @pl.when(z + r <= n - 1)
            def _():
                merge(z + r, k)

    for r in range(1, n):
        for k in range(nk):

            @pl.when(z >= r)
            def _():
                up_ag(z - r, k, r - 1).wait_recv()

                @pl.when(z < n - 1)
                def _():
                    up_ag(z - r, k, r).start()

            @pl.when(z + r <= n - 1)
            def _():
                dn_ag(z + r, k, r - 1).wait_recv()

                @pl.when(z > 0)
                def _():
                    dn_ag(z + r, k, r).start()

            @pl.when((z > 0) & (z < r))
            def _():
                h = n + z - r
                up_rs(h, k, r - 1).wait_recv()
                sbuf[h, k] = (part[h, k] + up_in[h, k].astype(F32)).astype(BF16)
                up_rs(h, k, r).start()

            @pl.when((z < n - 1) & (z + r > n - 1))
            def _():
                h = z + r - n
                dn_rs(h, k, r - 1).wait_recv()
                sbuf[h, k] = (part[h, k] + dn_in[h, k].astype(F32)).astype(BF16)
                dn_rs(h, k, r).start()

            @pl.when(z >= r)
            def _():
                weight_tile(z - r, k)

            @pl.when(z + r <= n - 1)
            def _():
                weight_tile(z + r, k)

            merge_round(r - 1, k)
            if r == n - 1 and k >= 2:
                merge_round(r, k - 2)
    for k in range(max(nk - 2, 0), nk):
        merge_round(n - 1, k)

    for k in range(1, chips):
        source = lax.rem(chip + k, chips)
        remote(
            bias.at[source], bias.at[source], bi_s.at[k], bi_r.at[source], lax.rem(dp + 2 * k, dpn), z
        ).wait_recv()
    total = bias[0]
    for k in range(1, chips):
        total = total + bias[k]
    bg_ref[...] = total[0]

    for k in range(nk):
        for j in range(2):
            rs = slice(k * lane + j * piece, k * lane + (j + 1) * piece)
            acc = wg_ref[rs, :]
            for role in range(2):
                remote(
                    wsend.at[along_x, k, j], wrecv.at[role, k, j], pl_s.at[0, k, j], pl_r.at[role, k, j],
                    partner, z,
                ).wait_recv()
                acc = acc + wrecv[role, k, j].astype(F32)
            wg_ref[rs, :] = acc

    for k in range(nk):

        @pl.when(z > 0)
        def _():
            up_rs(z, k, n - 1).wait_recv()
            part[z, k] += up_in[z, k].astype(F32)

        @pl.when(z < n - 1)
        def _():
            dn_rs(z, k, n - 1).wait_recv()
            part[z, k] += dn_in[z, k].astype(F32)

        at = slice(k * ptile, (k + 1) * ptile)
        xg_ref[:, at] = (part[z, k] * slope[:, at]).astype(BF16)

    raw_copy.wait_send()

    @pl.when(core == 1)
    def _():
        for c in tail_copies:
            c.wait_send()

    for c in range(1, chips):
        bias_copy(c).wait_send()
        h = lax.rem(chip + c, chips)
        for k in range(nk):
            for j in range(2):
                remote(
                    wsend.at[h, k, j], wrecv.at[0, k, j], pl_s.at[h, k, j], pl_r.at[0, k, j], partner, z
                ).wait_send()
    for k in range(nk):
        act_copy(k).wait_send()
        for r in range(n):

            @pl.when(z < n - 1)
            def _():
                up_rs(0, k, r).wait_send()

            @pl.when(z > 0)
            def _():
                dn_rs(0, k, r).wait_send()


def per_device_fast(n, dpn, grad_tokens, hidden_input, output_weight, image_tokens, moved_images):
    tok, cols = grad_tokens.shape
    rows, width = hidden_input.shape
    half = width // 2
    chips = dpn // 2
    lane = 128
    nk = half // lane
    ptile = width // nk
    dma = pltpu.SemaphoreType.DMA
    vmem = pl.BlockSpec(memory_space=pltpu.VMEM)
    return pl.pallas_call(
        functools.partial(kernel, n, dpn),
        out_shape=(
            jax.ShapeDtypeStruct((rows, width), BF16),
            jax.ShapeDtypeStruct((half, cols), F32),
            jax.ShapeDtypeStruct((cols,), F32),
        ),
        in_specs=[
            vmem, vmem, pl.BlockSpec(memory_space=pl.ANY), vmem, pl.BlockSpec(memory_space=pltpu.SMEM),
        ],
        out_specs=(vmem, vmem, vmem),
        scratch_shapes=[
            pltpu.VMEM(output_weight.shape, BF16),
            pltpu.VMEM((tok, cols), BF16),
            pltpu.VMEM((rows - tok, cols), BF16),
            pltpu.VMEM((n, nk, 2, rows, lane), BF16),
            pltpu.VMEM((nk, rows, lane), BF16),
            pltpu.VMEM((rows, width), F32),
            pltpu.VMEM((2, rows, cols), BF16),
            pltpu.VMEM((n, nk, rows, ptile), F32),
            pltpu.VMEM((n, nk, rows, ptile), BF16),
            pltpu.VMEM((n, nk, rows, ptile), BF16),
            pltpu.VMEM((n, nk, rows, ptile), BF16),
            pltpu.VMEM((chips, nk, 2, lane // 2, cols), BF16),
            pltpu.VMEM((2, nk, 2, lane // 2, cols), BF16),
            pltpu.VMEM((2, nk, lane // 2, cols), BF16),
            pltpu.VMEM((chips, 8, cols), F32),
            dma,
            dma,
            dma,
            dma((nk,)),
            dma((nk,)),
            dma((2,)),
            dma,
            dma((n, nk)),
            dma((n, nk)),
            dma((n, nk)),
            dma((n, nk)),
            dma((chips, nk, 2)),
            dma((2, nk, 2)),
            dma((2, nk)),
            dma((chips,)),
            dma((chips,)),
        ],
        compiler_params=pltpu.CompilerParams(
            collective_id=0, has_side_effects=True, vmem_limit_bytes=60 * 1024 * 1024
        ),
    )(grad_tokens, hidden_input, output_weight, image_tokens, moved_images)


def solution(mesh):
    n, dpn = mesh.shape["tensor"], mesh.shape["dp"]
    fast = dpn == 2 * n == 2 * 2 * 2
    return jax.shard_map(
        functools.partial(per_device_fast, n, dpn) if fast else per_device_any,
        mesh=mesh,
        in_specs=(P("dp", "tensor"), P("dp", "tensor"), P(None, "tensor"), P(), P()),
        out_specs=(P("dp", "tensor"), P("dp", "tensor"), P("tensor")),
        check_vma=False,
    )
```

profile of v0, /device:TPU:0, one launch (start us, length us, event | category | flops | bytes accessed | tf_op | source)
XLA Modules:
  0.0 72.4 jit_solution(8034197879788422284)
XLA Ops:
  0.6 68.1 %shard_map.76 = (bf16[256,1280]{1,0:T(8,128)(2,1)}, f32[640,512]{1,0:T(8,128)}, f32[512]{0:T(512)}) custom-call(bf16[192,512]{1,0:T(8,128)(2,1)} %g_ref.1, bf16[256,1280]{1,0:T(8,128)(2,1)} %x_ref.1, bf16[5120,512]{1,0:T(8,128)(2,1)} %w_hbm.1, s32[8,8]{1,0:T(8,128)} %it_ref.1, s32[8]{0:T(128)} %mv_ref.1), custom_call_target="tpu_custom_call" | custom-call | tf_op jit(solution)/shard_map/pallas_call | solution.py:464
  68.7 0.0 copy-start
  68.7 2.1 %copy.11 = bf16[256,1280]{1,0:T(8,128)(2,1)} copy(bf16[256,1280]{1,0:T(8,128)(2,1)} %get-tuple-element.6) | data formatting | bytes 1310720
  70.8 0.0 copy-done
  70.8 0.0 copy-start.1
  70.8 1.1 %copy.12 = f32[640,512]{1,0:T(8,128)} copy(f32[640,512]{1,0:T(8,128)S(1)} %copy-done) | data formatting | bytes 2621440
  71.8 0.0 copy-done.1
  71.8 0.6 copy.13
Async XLA Ops:
  68.7 2.1 %copy-start = (f32[640,512]{1,0:T(8,128)S(1)}, f32[640,512]{1,0:T(8,128)}, u32[]{:S(2)}) copy-start(f32[640,512]{1,0:T(8,128)} %get-tuple-element.7) | copy-start | bytes 3932164
  70.8 1.1 %copy-start.1 = (f32[512]{0:T(512)S(1)}, f32[512]{0:T(512)}, u32[]{:S(2)}) copy-start(f32[512]{0:T(512)} %get-tuple-element.8) | copy-start | bytes 6148
where the time goes:
time: 72.6 us; the launch traced here: 72.4 us
  Pallas kernels  68.1 us (94%)
  local copies, waits for them, and re-layouts  3.71 us (5%)
    pallas_call x1, Pallas kernels, per_device_fast(): pl.pallas_call(functools.partial(kernel, n, dpn), out_shape=(jax.ShapeDty...  68.1 us
    unnamed x7, local copies, waits for them, and re-layouts  3.71 us

commit v1 on v0

v1 whole, which is shorter than its diff:
```python
import functools

import jax
import jax.numpy as jnp
from jax import lax
from jax.experimental import pallas as pl
from jax.experimental.pallas import tpu as pltpu
from jax.sharding import PartitionSpec as P

root_half = 0.7071067811865476
inv_root_tau = 0.3989422804014327
MESH = pl.DeviceIdType.MESH
F32 = jnp.float32
BF16 = jnp.bfloat16


def from_behind(value, axis, steps):
    count = lax.axis_size(axis)
    pairs = [(source, (source + steps) % count) for source in range(count)]
    return lax.ppermute(value, axis, pairs)


def gelu_parts(values):
    normal_cdf = 0.5 * (1.0 + lax.erf(values * root_half))
    density = jnp.exp(-0.5 * values * values) * inv_root_tau
    return (values * normal_cdf, normal_cdf + values * density)


def kept_lengths(image_tokens, moved_images):
    present = jnp.sum((image_tokens > 0).astype(jnp.int32), axis=1)
    slot_ids = jnp.arange(image_tokens.shape[1], dtype=jnp.int32)
    kept_mask = slot_ids[None, :] < (present - moved_images)[:, None]
    return jnp.sum(jnp.where(kept_mask, image_tokens, 0), axis=1)


def per_device_any(grad_tokens, hidden_input, output_weight, image_tokens, moved_images):
    dp_count = lax.axis_size("dp")
    dp_index = lax.axis_index("dp")
    tok_rows = grad_tokens.shape[0]
    buffer_rows = hidden_input.shape[0]
    tail_count = buffer_rows - tok_rows
    keep_len = kept_lengths(image_tokens, moved_images)
    own_keep = jnp.sum(jnp.where(jnp.arange(dp_count, dtype=jnp.int32) == dp_index, keep_len, 0))
    positions = jnp.arange(tok_rows, dtype=jnp.int32)[:, None]
    zero_value = jnp.zeros((), BF16)
    kept_rows = jnp.where(positions < own_keep, grad_tokens, zero_value)
    moving = jnp.where(
        positions[tok_rows - tail_count :] >= own_keep,
        grad_tokens[tok_rows - tail_count :],
        zero_value,
    )
    arrived = from_behind(moving, "dp", 1)
    grad_rows = jnp.concatenate([kept_rows, arrived], axis=0)
    bias_grad = lax.psum(jnp.sum(grad_tokens.astype(F32), axis=0), "dp")
    activation, slopes = gelu_parts(hidden_input.astype(F32))
    partials = lax.dot_general(
        grad_rows, output_weight, (((1,), (1,)), ((), ())), preferred_element_type=F32
    )
    grad_hidden = lax.psum_scatter(
        partials.astype(BF16), "tensor", scatter_dimension=1, tiled=True
    ).astype(F32)
    input_grad = (grad_hidden * slopes).astype(BF16)
    full_act = lax.all_gather(activation.astype(BF16), "tensor", axis=1, tiled=True)
    hidden_width = full_act.shape[1]
    rows_each = (hidden_width + 8 * dp_count - 1) // (8 * dp_count) * 8
    padded = jnp.pad(full_act, ((0, 0), (0, rows_each * dp_count - hidden_width)))
    weight_grad = lax.psum_scatter(
        lax.dot_general(
            padded, grad_rows, (((0,), (0,)), ((), ())), preferred_element_type=F32
        ),
        "dp",
        scatter_dimension=0,
        tiled=True,
    )
    return (input_grad, weight_grad, bias_grad)


def kernel(
    n, dpn,
    g_hbm, x_hbm, w_hbm, it_hbm, mv_hbm,
    xg_ref, wg_ref, bg_ref,
    it_ref, mv_ref, w_ref, x_ref, xn, graw, act, act_other, slope, part, sbuf, up_in, dn_in, wsend, wrecv, wmid, bias,
    tsend, trecv,
    plan_sem, w_sem, x_sem, g_sem, core_s, core_r, act_s, act_r, xt_s, xt_r, tail_s, tail_r,
    up0_s, up0_r, dn0_s, dn0_r, up_s, up_r, dn_s, dn_r, pl_s, pl_r, mid_r, bi_s, bi_r,
):
    dp = lax.axis_index("dp")
    z = lax.axis_index("tensor")
    core = lax.rem(dp, 2)
    chip = lax.div(dp, 2)
    partner = dp + 1 - 2 * core
    after = lax.rem(dp + 1, dpn)
    before = lax.rem(dp + dpn - 1, dpn)
    chips = dpn // 2
    tok = g_hbm.shape[0]
    rows, width = x_hbm.shape
    half = width // 2
    tails = rows - tok
    main = tok - tails
    lane = 128
    nk = half // lane
    ptile = width // nk
    late = 2
    early = range(late, nk)
    main_rows = pl.ds(0, main)
    tail_rows = pl.ds(main, tails)
    slot_rows = pl.ds(tok, tails)

    x_copies = [
        pltpu.make_async_copy(x_hbm.at[slot_rows], x_ref.at[slot_rows], x_sem.at[0]),
        pltpu.make_async_copy(x_hbm.at[pl.ds(0, tok)], x_ref.at[pl.ds(0, tok)], x_sem.at[1]),
    ]
    g_copy = pltpu.make_async_copy(g_hbm, graw.at[core], g_sem)
    w_copy = pltpu.make_async_copy(w_hbm, w_ref, w_sem)
    plan_copies = [
        pltpu.make_async_copy(it_hbm, it_ref, plan_sem.at[0]),
        pltpu.make_async_copy(mv_hbm, mv_ref, plan_sem.at[1]),
    ]
    for c in x_copies + plan_copies:
        c.start()
    g_copy.start()
    w_copy.start()

    barrier = pltpu.get_barrier_semaphore()

    def greet(d, t):
        pl.semaphore_signal(barrier, inc=1, device_id=(d, t), device_id_type=MESH)

    for k in range(1, dpn):
        greet(lax.rem(dp + k, dpn), z)

    @pl.when(z > 0)
    def _():
        greet(dp, z - 1)
        greet(partner, z - 1)

    @pl.when(z < n - 1)
    def _():
        greet(dp, z + 1)
        greet(partner, z + 1)

    pl.semaphore_wait(barrier, dpn - 1 + jnp.where(z > 0, 2, 0) + jnp.where(z < n - 1, 2, 0))

    def remote(src, dst, ss, rs, d, t):
        return pltpu.make_async_remote_copy(
            src_ref=src, dst_ref=dst, send_sem=ss, recv_sem=rs, device_id=(d, t), device_id_type=MESH
        )

    x_tail_copy = remote(x_ref.at[slot_rows], xn, xt_s, xt_r, before, z)
    raw_copy = remote(graw.at[core], graw.at[core], core_s, core_r, partner, z)
    x_copies[0].wait()
    x_tail_copy.start()

    for c in plan_copies:
        c.wait()
    images = it_ref[pl.ds(dp, 1), :].astype(F32)
    present = jnp.sum(jnp.where(images > 0, 1.0, 0.0), axis=1, keepdims=True)
    ids = lax.broadcasted_iota(jnp.int32, images.shape, 1).astype(F32)
    keep = jnp.sum(
        jnp.where(ids < present - mv_ref[dp].astype(F32), images, 0.0), axis=1, keepdims=True
    )

    def stays(columns):
        return lax.broadcasted_iota(jnp.int32, (tails, columns), 0).astype(F32) + main < keep

    def pieces(k):
        if k < late:
            return [(k, 0, tok)]
        return [(k, 0, main), (nk + k - late, main, tails)]

    def act_copy(k, p, r0, rn):
        rs = pl.ds(r0, rn)
        return remote(act_other.at[k, rs], act.at[z, k, core, rs], act_s.at[p], act_r.at[p], partner, z)

    def first_copies(k, p, r0, rn, ss, rr, t):
        rs = pl.ds(r0, rn)
        target = act.at[z, k, core, rs]
        return (
            remote(target, target, ss.at[p, 0], rr.at[p, core], dp, t),
            remote(act_other.at[k, rs], target, ss.at[p, 1], rr.at[p, core], partner, t),
        )

    def send_first(k, p, r0, rn):
        @pl.when(z < n - 1)
        def _():
            for c in first_copies(k, p, r0, rn, up0_s, up0_r, z + 1):
                c.start()

        @pl.when(z > 0)
        def _():
            for c in first_copies(k, p, r0, rn, dn0_s, dn0_r, z - 1):
                c.start()

        act_copy(k, p, r0, rn).start()

    step_rows = 64

    def put(to_other, k, rs, a):
        if to_other:
            act_other[k, rs, :] = a
        else:
            act[z, k, core, rs, :] = a

    def normal_cdf(v):
        return 0.5 * (1.0 + lax.erf(v * root_half))

    def columns_of(which, k):
        return pl.ds(pl.multiple_of(which * half + k * lane, lane), lane)

    def gelu_main(k):
        for which, to_other in ((1 - core, True), (core, False)):
            cols = columns_of(which, k)

            def body(i, carry):
                rs = pl.ds(pl.multiple_of(i * step_rows, step_rows), step_rows)
                v = x_ref[rs, cols].astype(F32)
                cdf = normal_cdf(v)
                slope[rs, cols] = cdf
                put(to_other, k, rs, (v * cdf).astype(BF16))
                return carry

            lax.fori_loop(0, main // step_rows, body, 0)

    def gelu_tail(k):
        for which, to_other in ((1 - core, True), (core, False)):
            cols = columns_of(which, k)
            v = x_ref[tail_rows, cols].astype(F32)
            own = normal_cdf(v)
            slope[tail_rows, cols] = own
            u = xn[:, cols].astype(F32)
            other = normal_cdf(u)
            slope[slot_rows, cols] = other
            put(to_other, k, tail_rows, jnp.where(stays(lane), v * own, u * other).astype(BF16))

    x_copies[1].wait()
    for k in early:
        gelu_main(k)
        send_first(k, *pieces(k)[0])
    g_copy.wait()
    raw_copy.start()
    for k in range(late):
        gelu_main(k)
    x_tail_copy.wait_recv()
    for k in range(nk):
        gelu_tail(k)
        send_first(k, *pieces(k)[-1])

    def up_ag(h, k, r):
        return remote(act.at[h, k], act.at[h, k], up_s.at[r - 1, k], up_r.at[r - 1, k], dp, z + 1)

    def dn_ag(h, k, r):
        return remote(act.at[h, k], act.at[h, k], dn_s.at[r - 1, k], dn_r.at[r - 1, k], dp, z - 1)

    def rs_piece(ref, h, c):
        return ref.at[h, :, tail_rows] if c == 0 else ref.at[h, c - 1, main_rows]

    def up_rs(h, c, r):
        return remote(
            rs_piece(sbuf, h, c), rs_piece(up_in, h, c), up_s.at[r - 1, c], up_r.at[r - 1, c], dp, z + 1
        )

    def dn_rs(h, c, r):
        return remote(
            rs_piece(sbuf, h, c), rs_piece(dn_in, h, c), dn_s.at[r - 1, c], dn_r.at[r - 1, c], dp, z - 1
        )

    def add_up(h, c, extra):
        if c == 0:
            total = part[h, :, main:tok, :]
            if extra is not None:
                total = total + extra[h, :, main:tok, :].astype(F32)
            sbuf[h, :, main:tok, :] = total.astype(BF16)
        else:
            total = part[h, c - 1, 0:main, :]
            if extra is not None:
                total = total + extra[h, c - 1, 0:main, :].astype(F32)
            sbuf[h, c - 1, 0:main, :] = total.astype(BF16)

    w_copy.wait()

    def all_h(i, carry):
        h = lax.div(i, nk)
        k = lax.rem(i, nk)
        at = pl.ds(pl.multiple_of(i * ptile, ptile), ptile)
        part[h, k] = lax.dot_general(
            graw[core], w_ref[at, :], (((1,), (1,)), ((), ())), preferred_element_type=F32
        )
        return carry

    lax.fori_loop(0, n * nk, all_h, 0)

    @pl.when(z == 0)
    def _():
        for r in range(1, n):
            for c in range(nk + 1):
                add_up(n - r, c, None)
                up_rs(n - r, c, r).start()

    @pl.when(z == n - 1)
    def _():
        for r in range(1, n):
            for c in range(nk + 1):
                add_up(r - 1, c, None)
                dn_rs(r - 1, c, r).start()

    raw_copy.wait_recv()
    chip_sum = jnp.sum(graw[0].astype(F32), axis=0, keepdims=True) + jnp.sum(
        graw[1].astype(F32), axis=0, keepdims=True
    )
    bias[chip] = jnp.broadcast_to(chip_sum, bias.shape[1:])

    def bias_copy(k):
        return remote(
            bias.at[chip], bias.at[chip], bi_s.at[k], bi_r.at[chip], lax.rem(dp + 2 * k, dpn), z
        )

    for k in range(1, chips):
        bias_copy(k).start()

    piece = lane // 2

    def relation(h):
        return jnp.where(lax.rem(chip, 2) != lax.rem(h, 2), 1, 0) + jnp.where(
            lax.div(chip, 2) != lax.div(h, 2), 2, 0
        )

    along_x = chip + 1 - 2 * lax.rem(chip, 2)
    along_y = lax.rem(chip + 2, chips)

    def owner_copy(h, k, j):
        role = relation(h) - 1
        return remote(
            wsend.at[h, k, j], wrecv.at[role, k, j], pl_s.at[h, k, j], pl_r.at[role, k, j], h * 2 + core, z
        )

    def corner_copy(h, k, j):
        through = along_x if j == 0 else along_y
        return remote(
            wsend.at[h, k, j], wmid.at[1 - j, k], pl_s.at[h, k, j], mid_r.at[1 - j, k], through * 2 + core, z
        )

    def merge(h, k):
        rel = relation(h)
        for role in (1, 2):
            over = 1 if role == 1 else 0

            @pl.when(rel == role)
            def _():
                corner_copy(h, k, over).wait_recv()
                wsend[h, k, over] = (
                    wsend[h, k, over].astype(F32) + wmid[role - 1, k].astype(F32)
                ).astype(BF16)
                owner_copy(h, k, over).start()

    def weight_tile(h, k):
        acc = lax.dot_general(
            act[h, k].reshape(2 * tok, lane),
            graw[...].reshape(2 * tok, graw.shape[2]),
            (((0,), (0,)), ((), ())),
            preferred_element_type=F32,
        )
        rel = relation(h)

        @pl.when(rel == 0)
        def _():
            wg_ref[k * lane : (k + 1) * lane, :] = acc

        @pl.when(rel != 0)
        def _():
            for j in range(2):
                wsend[h, k, j] = acc[j * piece : (j + 1) * piece].astype(BF16)

        @pl.when(rel == 1)
        def _():
            owner_copy(h, k, 0).start()

        @pl.when(rel == 2)
        def _():
            owner_copy(h, k, 1).start()

        @pl.when(rel == 3)
        def _():
            for j in range(2):
                corner_copy(h, k, j).start()

    for k in range(nk):
        for p, r0, rn in pieces(k):
            act_copy(k, p, r0, rn).wait_recv()
        weight_tile(z, k)

    def merge_round(r, k):
        if r == 0:
            merge(z, k)
        else:

            @pl.when(z >= r)
            def _():
                merge(z - r, k)

            @pl.when(z + r <= n - 1)
            def _():
                merge(z + r, k)

    def first_arrivals(h, k, ss, rr):
        for p, r0, rn in pieces(k):
            rs = pl.ds(r0, rn)
            for s in range(2):
                remote(
                    act.at[h, k, s, rs], act.at[h, k, s, rs], ss.at[p, 0], rr.at[p, s], partner, z
                ).wait_recv()

    def finish_slope(k):
        at = slice(k * ptile, (k + 1) * ptile)

        def grow(source, source_rows, target_rows):
            v = source[source_rows, at].astype(F32)
            slope[target_rows, at] += v * (jnp.exp(-0.5 * v * v) * inv_root_tau)

        def body(i, carry):
            rs = pl.ds(pl.multiple_of(i * step_rows, step_rows), step_rows)
            grow(x_ref, rs, rs)
            return carry

        lax.fori_loop(0, tok // step_rows, body, 0)
        grow(xn, pl.ds(0, tails), slot_rows)

    for r in range(1, n):
        for c in range(nk + 1):
            if c < nk:

                @pl.when(z >= r)
                def _():
                    if r == 1:
                        first_arrivals(z - 1, c, up0_s, up0_r)
                    else:
                        up_ag(z - r, c, r - 1).wait_recv()

                    @pl.when(z < n - 1)
                    def _():
                        up_ag(z - r, c, r).start()

                @pl.when(z + r <= n - 1)
                def _():
                    if r == 1:
                        first_arrivals(z + 1, c, dn0_s, dn0_r)
                    else:
                        dn_ag(z + r, c, r - 1).wait_recv()

                    @pl.when(z > 0)
                    def _():
                        dn_ag(z + r, c, r).start()

            if r > 1:

                @pl.when((z > 0) & (z < r))
                def _():
                    h = n + z - r
                    up_rs(h, c, r - 1).wait_recv()
                    add_up(h, c, up_in)
                    up_rs(h, c, r).start()

                @pl.when((z < n - 1) & (z + r > n - 1))
                def _():
                    h = z + r - n
                    dn_rs(h, c, r - 1).wait_recv()
                    add_up(h, c, dn_in)
                    dn_rs(h, c, r).start()

            if c < nk:

                @pl.when(z >= r)
                def _():
                    weight_tile(z - r, c)

                @pl.when(z + r <= n - 1)
                def _():
                    weight_tile(z + r, c)

                merge_round(r - 1, c)
                if r == 1:
                    finish_slope(c)
                if r == n - 1 and c >= 2:
                    merge_round(r, c - 2)
    for k in range(max(nk - 2, 0), nk):
        merge_round(n - 1, k)

    def last_sum(c):
        index = slice(main, tok) if c == 0 else slice(0, main)
        which = slice(None) if c == 0 else c - 1

        @pl.when(z > 0)
        def _():
            up_rs(z, c, n - 1).wait_recv()
            part[z, which, index, :] += up_in[z, which, index, :].astype(F32)

        @pl.when(z < n - 1)
        def _():
            dn_rs(z, c, n - 1).wait_recv()
            part[z, which, index, :] += dn_in[z, which, index, :].astype(F32)

    last_sum(0)
    zero = jnp.zeros((), F32)
    for k in range(nk):
        at = slice(k * ptile, (k + 1) * ptile)
        total = part[z, k, main:tok, :]
        here = stays(ptile)
        xg_ref[main:tok, at] = jnp.where(here, total * slope[main:tok, at], zero).astype(BF16)
        tsend[:, at] = jnp.where(here, zero, total * slope[tok:rows, at]).astype(BF16)
    tail_copy = remote(tsend, trecv, tail_s, tail_r, after, z)
    tail_copy.start()

    for k in range(1, chips):
        source = lax.rem(chip + k, chips)
        remote(
            bias.at[source], bias.at[source], bi_s.at[k], bi_r.at[source], lax.rem(dp + 2 * k, dpn), z
        ).wait_recv()
    total = bias[0]
    for k in range(1, chips):
        total = total + bias[k]
    bg_ref[...] = total[0]

    for k in range(nk):
        for j in range(2):
            rs = slice(k * lane + j * piece, k * lane + (j + 1) * piece)
            acc = wg_ref[rs, :]
            for role in range(2):
                remote(
                    wsend.at[along_x, k, j], wrecv.at[role, k, j], pl_s.at[0, k, j], pl_r.at[role, k, j],
                    partner, z,
                ).wait_recv()
                acc = acc + wrecv[role, k, j].astype(F32)
            wg_ref[rs, :] = acc

    for k in range(nk):
        last_sum(k + 1)
        at = slice(k * ptile, (k + 1) * ptile)
        xg_ref[0:main, at] = (part[z, k, 0:main, :] * slope[0:main, at]).astype(BF16)

    tail_copy.wait_recv()
    xg_ref[tok:rows, :] = trecv[...]

    tail_copy.wait_send()
    x_tail_copy.wait_send()
    raw_copy.wait_send()
    for c in range(1, chips):
        bias_copy(c).wait_send()
        h = lax.rem(chip + c, chips)
        for k in range(nk):
            for j in range(2):
                remote(
                    wsend.at[h, k, j], wrecv.at[0, k, j], pl_s.at[h, k, j], pl_r.at[0, k, j], partner, z
                ).wait_send()
    for k in range(nk):
        for p in pieces(k):
            act_copy(k, *p).wait_send()

            @pl.when(z < n - 1)
            def _():
                for c in first_copies(k, *p, up0_s, up0_r, z + 1):
                    c.wait_send()

            @pl.when(z > 0)
            def _():
                for c in first_copies(k, *p, dn0_s, dn0_r, z - 1):
                    c.wait_send()

    for r in range(1, n):

        @pl.when((z < n - 1) & (z >= r))
        def _():
            for k in range(nk):
                up_ag(0, k, r).wait_send()

        @pl.when((z < n - 1) & (z < r))
        def _():
            for c in range(nk + 1):
                up_rs(0, c, r).wait_send()

        @pl.when((z > 0) & (z + r <= n - 1))
        def _():
            for k in range(nk):
                dn_ag(0, k, r).wait_send()

        @pl.when((z > 0) & (z + r > n - 1))
        def _():
            for c in range(nk + 1):
                dn_rs(0, c, r).wait_send()


def per_device_fast(n, dpn, grad_tokens, hidden_input, output_weight, image_tokens, moved_images):
    tok, cols = grad_tokens.shape
    rows, width = hidden_input.shape
    half = width // 2
    chips = dpn // 2
    lane = 128
    nk = half // lane
    ptile = width // nk
    npiece = 2 * nk - 2
    dma = pltpu.SemaphoreType.DMA
    vmem = pl.BlockSpec(memory_space=pltpu.VMEM)
    hbm = pl.BlockSpec(memory_space=pltpu.HBM)
    return pl.pallas_call(
        functools.partial(kernel, n, dpn),
        out_shape=(
            jax.ShapeDtypeStruct((rows, width), BF16),
            jax.ShapeDtypeStruct((half, cols), F32),
            jax.ShapeDtypeStruct((cols,), F32),
        ),
        in_specs=[hbm] * 5,
        out_specs=(vmem, vmem, vmem),
        scratch_shapes=[
            pltpu.VMEM(image_tokens.shape, jnp.int32),
            pltpu.SMEM(moved_images.shape, jnp.int32),
            pltpu.VMEM(output_weight.shape, BF16),
            pltpu.VMEM((rows, width), BF16),
            pltpu.VMEM((rows - tok, width), BF16),
            pltpu.VMEM((2, tok, cols), BF16),
            pltpu.VMEM((n, nk, 2, tok, lane), BF16),
            pltpu.VMEM((nk, tok, lane), BF16),
            pltpu.VMEM((rows, width), F32),
            pltpu.VMEM((n, nk, tok, ptile), F32),
            pltpu.VMEM((n, nk, tok, ptile), BF16),
            pltpu.VMEM((n, nk, tok, ptile), BF16),
            pltpu.VMEM((n, nk, tok, ptile), BF16),
            pltpu.VMEM((chips, nk, 2, lane // 2, cols), BF16),
            pltpu.VMEM((2, nk, 2, lane // 2, cols), BF16),
            pltpu.VMEM((2, nk, lane // 2, cols), BF16),
            pltpu.VMEM((chips, 8, cols), F32),
            pltpu.VMEM((rows - tok, width), BF16),
            pltpu.VMEM((rows - tok, width), BF16),
            dma((2,)),
            dma,
            dma((2,)),
            dma,
            dma,
            dma,
            dma((npiece,)),
            dma((npiece,)),
            dma,
            dma,
            dma,
            dma,
            dma((npiece, 2)),
            dma((npiece, 2)),
            dma((npiece, 2)),
            dma((npiece, 2)),
            dma((n - 1, nk + 1)),
            dma((n - 1, nk + 1)),
            dma((n - 1, nk + 1)),
            dma((n - 1, nk + 1)),
            dma((chips, nk, 2)),
            dma((2, nk, 2)),
            dma((2, nk)),
            dma((chips,)),
            dma((chips,)),
        ],
        compiler_params=pltpu.CompilerParams(
            collective_id=0, has_side_effects=True, vmem_limit_bytes=48 * 1024 * 1024
        ),
    )(grad_tokens, hidden_input, output_weight, image_tokens, moved_images)


def solution(mesh):
    n, dpn = mesh.shape["tensor"], mesh.shape["dp"]
    fast = dpn == 2 * n == 2 * 2 * 2
    return jax.shard_map(
        functools.partial(per_device_fast, n, dpn) if fast else per_device_any,
        mesh=mesh,
        in_specs=(P("dp", "tensor"), P("dp", "tensor"), P(None, "tensor"), P(), P()),
        out_specs=(P("dp", "tensor"), P("dp", "tensor"), P("tensor")),
        check_vma=False,
    )
```

time: 72.6 us -> 60.7 us (0.84)
  the two profiles are of different devices: /device:TPU:0 before, /device:TPU:6 now
where the time goes in v1:
time: 60.7 us; the launch traced here: 60.5 us
  Pallas kernels  54 us (89%)
  local copies, waits for them, and re-layouts  5.82 us (10%)
  between operations  0.65 us (1%)
    pallas_call x1, Pallas kernels, per_device_fast(): pl.pallas_call(functools.partial(kernel, n, dpn), out_shape=(jax.ShapeDty...  54 us
    unnamed x11, local copies, waits for them, and re-layouts  5.82 us

profile of v1, /device:TPU:6, one launch (start us, length us, event | category | flops | bytes accessed | tf_op | source)
XLA Modules:
  0.0 60.5 jit_solution(2951710615015712734)
XLA Ops:
  0.6 0.0 copy-start
  0.6 1.1 %copy-done = bf16[256,1280]{1,0:T(8,128)(2,1)S(1)} copy-done((bf16[256,1280]{1,0:T(8,128)(2,1)S(1)}, bf16[256,1280]{1,0:T(8,128)(2,1)}, u32[]{:S(2)}) %copy-start) | copy-done | bytes 655384
  1.7 0.0 copy-start.1
  1.7 0.9 %copy-done.1 = bf16[192,512]{1,0:T(8,128)(2,1)S(1)} copy-done((bf16[192,512]{1,0:T(8,128)(2,1)S(1)}, bf16[192,512]{1,0:T(8,128)(2,1)}, u32[]{:S(2)}) %copy-start.1) | copy-done | bytes 196632
  2.6 0.0 copy-start.2
  2.6 0.7 %copy-done.2 = s32[8,8]{1,0:T(8,128)S(1)} copy-done((s32[8,8]{1,0:T(8,128)S(1)}, s32[8,8]{1,0:T(8,128)}, u32[]{:S(2)}) %copy-start.2) | copy-done | bytes 280
  3.3 0.0 copy-start.3
  3.3 0.7 %copy-done.3 = s32[8]{0:T(128)S(1)} copy-done((s32[8]{0:T(128)S(1)}, s32[8]{0:T(128)}, u32[]{:S(2)}) %copy-start.3) | copy-done | bytes 56
  4.0 54.0 %shard_map.76 = (bf16[256,1280]{1,0:T(8,128)(2,1)S(1)}, f32[640,512]{1,0:T(8,128)S(1)}, f32[512]{0:T(512)S(1)}) custom-call(bf16[192,512]{1,0:T(8,128)(2,1)S(1)} %copy-done.1, bf16[256,1280]{1,0:T(8,128)(2,1)S(1)} %copy-done, bf16[5120,512]{1,0:T(8,128)(2,1)} %w_hbm.1, s32[8,8]{1,0:T(8,128)S(1)} %copy-done.2, s32[8]{0:T(128)S(1)} %copy-done.3), custom_call_target="tpu_custom_call" | custom-call | tf_op jit(solution)/shard_map/pallas_call | solution.py:602
  58.0 0.8 %copy.11 = bf16[256,1280]{1,0:T(8,128)(2,1)} copy(bf16[256,1280]{1,0:T(8,128)(2,1)S(1)} %get-tuple-element.6) | data formatting | bytes 1310720
  58.9 1.1 %copy.12 = f32[640,512]{1,0:T(8,128)} copy(f32[640,512]{1,0:T(8,128)S(1)} %get-tuple-element.7) | data formatting | bytes 2621440
  59.9 0.6 copy.13
Async XLA Ops:
  0.6 1.1 %copy-start = (bf16[256,1280]{1,0:T(8,128)(2,1)S(1)}, bf16[256,1280]{1,0:T(8,128)(2,1)}, u32[]{:S(2)}) copy-start(bf16[256,1280]{1,0:T(8,128)(2,1)} %x_hbm.1) | copy-start | bytes 1966084
  1.7 0.9 %copy-start.1 = (bf16[192,512]{1,0:T(8,128)(2,1)S(1)}, bf16[192,512]{1,0:T(8,128)(2,1)}, u32[]{:S(2)}) copy-start(bf16[192,512]{1,0:T(8,128)(2,1)} %g_hbm.1) | copy-start | bytes 589828
  2.6 0.7 %copy-start.2 = (s32[8,8]{1,0:T(8,128)S(1)}, s32[8,8]{1,0:T(8,128)}, u32[]{:S(2)}) copy-start(s32[8,8]{1,0:T(8,128)} %it_hbm.1) | copy-start | bytes 772
  3.3 0.7 %copy-start.3 = (s32[8]{0:T(128)S(1)}, s32[8]{0:T(128)}, u32[]{:S(2)}) copy-start(s32[8]{0:T(128)} %mv_hbm.1) | copy-start | bytes 100

commit v2 on v1

--- a/solution.py
+++ b/solution.py
@@ -587,7 +587,33 @@
                 dn_rs(0, c, r).wait_send()
 
 
-def per_device_fast(n, dpn, grad_tokens, hidden_input, output_weight, image_tokens, moved_images):
+def writer(a_ref, b_ref, c_ref, a_out, b_out, c_out, sems):
+    copies = [
+        pltpu.make_async_copy(b_ref, b_out, sems.at[0]),
+        pltpu.make_async_copy(a_ref, a_out, sems.at[1]),
+        pltpu.make_async_copy(c_ref, c_out, sems.at[2]),
+    ]
+    for c in copies:
+        c.start()
+    for c in copies:
+        c.wait()
+
+
+def write_out(*args):
+    vmem = pl.BlockSpec(memory_space=pltpu.VMEM)
+    hbm = pl.BlockSpec(memory_space=pltpu.HBM)
+    return pl.pallas_call(
+        writer,
+        out_shape=tuple(jax.ShapeDtypeStruct(a.shape, a.dtype) for a in args),
+        in_specs=[vmem] * len(args),
+        out_specs=tuple([hbm] * len(args)),
+        scratch_shapes=[pltpu.SemaphoreType.DMA((len(args),))],
+        compiler_params=pltpu.CompilerParams(vmem_limit_bytes=1024 * 1024),
+    )(*(pltpu.with_memory_space_constraint(a, pltpu.VMEM) for a in args))
+
+
+def per_device_fast(n, dpn, *args):
+    grad_tokens, hidden_input, output_weight, image_tokens, moved_images = args
     tok, cols = grad_tokens.shape
     rows, width = hidden_input.shape
     half = width // 2
@@ -599,7 +625,7 @@
     dma = pltpu.SemaphoreType.DMA
     vmem = pl.BlockSpec(memory_space=pltpu.VMEM)
     hbm = pl.BlockSpec(memory_space=pltpu.HBM)
-    return pl.pallas_call(
+    results = pl.pallas_call(
         functools.partial(kernel, n, dpn),
         out_shape=(
             jax.ShapeDtypeStruct((rows, width), BF16),
@@ -657,7 +683,8 @@
         compiler_params=pltpu.CompilerParams(
             collective_id=0, has_side_effects=True, vmem_limit_bytes=48 * 1024 * 1024
         ),
-    )(grad_tokens, hidden_input, output_weight, image_tokens, moved_images)
+    )(*(pltpu.with_memory_space_constraint(a, pltpu.HBM) for a in args))
+    return write_out(*results)
 
 
 def solution(mesh):

time: 60.7 us -> 55.4 us (0.913)
  local copies, waits for them, and re-layouts: 5.82 us -> 0 us
    unnamed x11 -> x0, local copies, waits for them, and re-layouts: 5.82 us -> none
    pallas_call x0 -> x1, Pallas kernels: none -> 1.3 us  [write_out(): pl.pallas_call(writer, out_shape=tuple((jax.ShapeDtypeStruct(a.shape, a.d...]
    pallas_call x1, Pallas kernels: 54 us -> 53.3 us  [per_device_fast(): pl.pallas_call(functools.partial(kernel, n, dpn), out_shape=(jax.ShapeDty...]
where the time goes in v2:
time: 55.4 us; the launch traced here: 55.3 us
  Pallas kernels  54.6 us (99%)
  between operations  0.64 us (1%)
    pallas_call x1, Pallas kernels, per_device_fast(): pl.pallas_call(functools.partial(kernel, n, dpn), out_shape=(jax.ShapeDty...  53.3 us
    pallas_call x1, Pallas kernels, write_out(): pl.pallas_call(writer, out_shape=tuple((jax.ShapeDtypeStruct(a.shape, a.d...  1.3 us

profile of v2, /device:TPU:6, one launch (start us, length us, event | category | flops | bytes accessed | tf_op | source)
XLA Modules:
  0.0 55.3 jit_solution(8671205966744555637)
XLA Ops:
  0.6 53.3 %shard_map.76 = (bf16[256,1280]{1,0:T(8,128)(2,1)S(1)}, f32[640,512]{1,0:T(8,128)S(1)}, f32[512]{0:T(512)S(1)}) custom-call(bf16[192,512]{1,0:T(8,128)(2,1)} %g_hbm.1, bf16[256,1280]{1,0:T(8,128)(2,1)} %x_hbm.1, bf16[5120,512]{1,0:T(8,128)(2,1)} %w_hbm.1, s32[8,8]{1,0:T(8,128)} %it_hbm.1, s32[8]{0:T(128)} %mv_hbm.1), custom_call_target="tpu_custom_call" | custom-call | tf_op jit(solution)/shard_map/pallas_call | solution.py:628
  54.0 1.3 %shard_map.77 = (bf16[256,1280]{1,0:T(8,128)(2,1)}, f32[640,512]{1,0:T(8,128)}, f32[512]{0:T(512)}) custom-call(bf16[256,1280]{1,0:T(8,128)(2,1)S(1)} %get-tuple-element.6.a_ref, f32[640,512]{1,0:T(8,128)S(1)} %get-tuple-element.7.b_ref, f32[512]{0:T(512)S(1)} %get-tuple-element.8.c_ref), custom_call_target="tpu_custom_call" | custom-call | tf_op jit(solution)/shard_map/pallas_call | solution.py:605

commit v3 on v2

--- a/solution.py
+++ b/solution.py
@@ -424,6 +424,46 @@
         lax.fori_loop(0, tok // step_rows, body, 0)
         grow(xn, pl.ds(0, tails), slot_rows)
 
+    def pass_up(c, r):
+        h = n + z - r
+        up_rs(h, c, r - 1).wait_recv()
+        add_up(h, c, up_in)
+        up_rs(h, c, r).start()
+
+    def pass_dn(c, r):
+        h = z + r - n
+        dn_rs(h, c, r - 1).wait_recv()
+        add_up(h, c, dn_in)
+        dn_rs(h, c, r).start()
+
+    def last_sum(c):
+        index = slice(main, tok) if c == 0 else slice(0, main)
+        which = slice(None) if c == 0 else c - 1
+
+        @pl.when(z > 0)
+        def _():
+            up_rs(z, c, n - 1).wait_recv()
+            part[z, which, index, :] += up_in[z, which, index, :].astype(F32)
+
+        @pl.when(z < n - 1)
+        def _():
+            dn_rs(z, c, n - 1).wait_recv()
+            part[z, which, index, :] += dn_in[z, which, index, :].astype(F32)
+
+    tail_copy = remote(tsend, trecv, tail_s, tail_r, after, z)
+
+    def finish_tail():
+        last_sum(0)
+        zero = jnp.zeros((), F32)
+        for k in range(nk):
+            at = slice(k * ptile, (k + 1) * ptile)
+            total = part[z, k, main:tok, :]
+            here = stays(ptile)
+            xg_ref[main:tok, at] = jnp.where(here, total * slope[main:tok, at], zero).astype(BF16)
+            tsend[:, at] = jnp.where(here, zero, total * slope[tok:rows, at]).astype(BF16)
+        tail_copy.start()
+
+    merge_after = {0: [], 1: [0], 2: [1], 3: [], 4: [2], 5: [3, 4]}
     for r in range(1, n):
         for c in range(nk + 1):
             if c < nk:
@@ -451,20 +491,15 @@
                         dn_ag(z + r, c, r).start()
 
             if r > 1:
-
-                @pl.when((z > 0) & (z < r))
+                last = r if c > 0 else r - 1
+
+                @pl.when((z > 0) & (z < last))
                 def _():
-                    h = n + z - r
-                    up_rs(h, c, r - 1).wait_recv()
-                    add_up(h, c, up_in)
-                    up_rs(h, c, r).start()
-
-                @pl.when((z < n - 1) & (z + r > n - 1))
+                    pass_up(c, r)
+
+                @pl.when((z < n - 1) & (z + last > n - 1))
                 def _():
-                    h = z + r - n
-                    dn_rs(h, c, r - 1).wait_recv()
-                    add_up(h, c, dn_in)
-                    dn_rs(h, c, r).start()
+                    pass_dn(c, r)
 
             if c < nk:
 
@@ -479,35 +514,29 @@
                 merge_round(r - 1, c)
                 if r == 1:
                     finish_slope(c)
-                if r == n - 1 and c >= 2:
-                    merge_round(r, c - 2)
-    for k in range(max(nk - 2, 0), nk):
-        merge_round(n - 1, k)
-
-    def last_sum(c):
-        index = slice(main, tok) if c == 0 else slice(0, main)
-        which = slice(None) if c == 0 else c - 1
-
-        @pl.when(z > 0)
-        def _():
-            up_rs(z, c, n - 1).wait_recv()
-            part[z, which, index, :] += up_in[z, which, index, :].astype(F32)
-
-        @pl.when(z < n - 1)
-        def _():
-            dn_rs(z, c, n - 1).wait_recv()
-            part[z, which, index, :] += dn_in[z, which, index, :].astype(F32)
-
-    last_sum(0)
-    zero = jnp.zeros((), F32)
-    for k in range(nk):
-        at = slice(k * ptile, (k + 1) * ptile)
-        total = part[z, k, main:tok, :]
-        here = stays(ptile)
-        xg_ref[main:tok, at] = jnp.where(here, total * slope[main:tok, at], zero).astype(BF16)
-        tsend[:, at] = jnp.where(here, zero, total * slope[tok:rows, at]).astype(BF16)
-    tail_copy = remote(tsend, trecv, tail_s, tail_r, after, z)
-    tail_copy.start()
+            if r < n - 1 and c == nk - 2 - r:
+
+                @pl.when(z == r)
+                def _():
+                    pass_up(0, r + 1)
+
+                @pl.when(z == n - 1 - r)
+                def _():
+                    pass_dn(0, r + 1)
+
+            if r == n - 1:
+                for k in merge_after[c]:
+                    merge_round(r, k)
+                if c == 1:
+
+                    @pl.when((z == 0) | (z == n - 1))
+                    def _():
+                        finish_tail()
+
+
+    @pl.when((z > 0) & (z < n - 1))
+    def _():
+        finish_tail()
 
     for k in range(1, chips):
         source = lax.rem(chip + k, chips)

time: 55.4 us -> 54.7 us (0.987)
  the two profiles are of different devices: /device:TPU:6 before, /device:TPU:7 now
where the time goes in v3:
time: 54.7 us; the launch traced here: 53.9 us
  Pallas kernels  53.2 us (97%)
  between operations  0.64 us (1%)
    pallas_call x1, Pallas kernels, per_device_fast(): pl.pallas_call(functools.partial(kernel, n, dpn), out_shape=(jax.ShapeDty...  51.9 us
    pallas_call x1, Pallas kernels, write_out(): pl.pallas_call(writer, out_shape=tuple((jax.ShapeDtypeStruct(a.shape, a.d...  1.3 us

profile of v3, /device:TPU:7, one launch (start us, length us, event | category | flops | bytes accessed | tf_op | source)
XLA Modules:
  0.0 53.9 jit_solution(7288911975914009105)
XLA Ops:
  0.6 51.9 %shard_map.76 = (bf16[256,1280]{1,0:T(8,128)(2,1)S(1)}, f32[640,512]{1,0:T(8,128)S(1)}, f32[512]{0:T(512)S(1)}) custom-call(bf16[192,512]{1,0:T(8,128)(2,1)} %g_hbm.1, bf16[256,1280]{1,0:T(8,128)(2,1)} %x_hbm.1, bf16[5120,512]{1,0:T(8,128)(2,1)} %w_hbm.1, s32[8,8]{1,0:T(8,128)} %it_hbm.1, s32[8]{0:T(128)} %mv_hbm.1), custom_call_target="tpu_custom_call" | custom-call | tf_op jit(solution)/shard_map/pallas_call | solution.py:657
  52.6 1.3 %shard_map.77 = (bf16[256,1280]{1,0:T(8,128)(2,1)}, f32[640,512]{1,0:T(8,128)}, f32[512]{0:T(512)}) custom-call(bf16[256,1280]{1,0:T(8,128)(2,1)S(1)} %get-tuple-element.6.a_ref, f32[640,512]{1,0:T(8,128)S(1)} %get-tuple-element.7.b_ref, f32[512]{0:T(512)S(1)} %get-tuple-element.8.c_ref), custom_call_target="tpu_custom_call" | custom-call | tf_op jit(solution)/shard_map/pallas_call | solution.py:634

commit v4 on v3

--- a/solution.py
+++ b/solution.py
@@ -463,7 +463,7 @@
             tsend[:, at] = jnp.where(here, zero, total * slope[tok:rows, at]).astype(BF16)
         tail_copy.start()
 
-    merge_after = {0: [], 1: [0], 2: [1], 3: [], 4: [2], 5: [3, 4]}
+    merge_after = {0: [], 1: [], 2: [0], 3: [1], 4: [2], 5: [3, 4]}
     for r in range(1, n):
         for c in range(nk + 1):
             if c < nk:
@@ -514,7 +514,7 @@
                 merge_round(r - 1, c)
                 if r == 1:
                     finish_slope(c)
-            if r < n - 1 and c == nk - 2 - r:
+            if r < n - 1 and c == (4 if r == 1 else 4):
 
                 @pl.when(z == r)
                 def _():
@@ -527,7 +527,7 @@
             if r == n - 1:
                 for k in merge_after[c]:
                     merge_round(r, k)
-                if c == 1:
+                if c == 4:
 
                     @pl.when((z == 0) | (z == n - 1))
                     def _():

time: 54.7 us -> 53.9 us (0.985); the launches traced: 53.9 us -> 53.7 us
  no operation moved by 1% of the time
where the time goes in v4:
time: 53.9 us; the launch traced here: 53.7 us
  Pallas kernels  53.1 us (99%)
  between operations  0.64 us (1%)
    pallas_call x1, Pallas kernels, per_device_fast(): pl.pallas_call(functools.partial(kernel, n, dpn), out_shape=(jax.ShapeDty...  51.8 us
    pallas_call x1, Pallas kernels, write_out(): pl.pallas_call(writer, out_shape=tuple((jax.ShapeDtypeStruct(a.shape, a.d...  1.3 us

profile of v4, /device:TPU:7, one launch (start us, length us, event | category | flops | bytes accessed | tf_op | source)
XLA Modules:
  0.0 53.7 jit_solution(5001947875002640570)
XLA Ops:
  0.6 51.8 %shard_map.76 = (bf16[256,1280]{1,0:T(8,128)(2,1)S(1)}, f32[640,512]{1,0:T(8,128)S(1)}, f32[512]{0:T(512)S(1)}) custom-call(bf16[192,512]{1,0:T(8,128)(2,1)} %g_hbm.1, bf16[256,1280]{1,0:T(8,128)(2,1)} %x_hbm.1, bf16[5120,512]{1,0:T(8,128)(2,1)} %w_hbm.1, s32[8,8]{1,0:T(8,128)} %it_hbm.1, s32[8]{0:T(128)} %mv_hbm.1), custom_call_target="tpu_custom_call" | custom-call | tf_op jit(solution)/shard_map/pallas_call | solution.py:657
  52.4 1.3 %shard_map.77 = (bf16[256,1280]{1,0:T(8,128)(2,1)}, f32[640,512]{1,0:T(8,128)}, f32[512]{0:T(512)}) custom-call(bf16[256,1280]{1,0:T(8,128)(2,1)S(1)} %get-tuple-element.6.a_ref, f32[640,512]{1,0:T(8,128)S(1)} %get-tuple-element.7.b_ref, f32[512]{0:T(512)S(1)} %get-tuple-element.8.c_ref), custom_call_target="tpu_custom_call" | custom-call | tf_op jit(solution)/shard_map/pallas_call | solution.py:634

commit v5 on v4

--- a/solution.py
+++ b/solution.py
@@ -463,7 +463,7 @@
             tsend[:, at] = jnp.where(here, zero, total * slope[tok:rows, at]).astype(BF16)
         tail_copy.start()
 
-    merge_after = {0: [], 1: [], 2: [0], 3: [1], 4: [2], 5: [3, 4]}
+    merge_after = {0: [], 1: [], 2: [0], 3: [1], 4: [], 5: [2, 3, 4]}
     for r in range(1, n):
         for c in range(nk + 1):
             if c < nk:

time: 53.9 us -> 53.9 us (level)
  no operation moved by 1% of the time
where the time goes in v5:
time: 53.9 us; the launch traced here: 53.7 us
  Pallas kernels  53.1 us (99%)
  between operations  0.64 us (1%)
    pallas_call x1, Pallas kernels, per_device_fast(): pl.pallas_call(functools.partial(kernel, n, dpn), out_shape=(jax.ShapeDty...  51.8 us
    pallas_call x1, Pallas kernels, write_out(): pl.pallas_call(writer, out_shape=tuple((jax.ShapeDtypeStruct(a.shape, a.d...  1.3 us

profile of v5, /device:TPU:7, one launch (start us, length us, event | category | flops | bytes accessed | tf_op | source)
XLA Modules:
  0.0 53.7 jit_solution(1142819386759798828)
XLA Ops:
  0.6 51.8 %shard_map.76 = (bf16[256,1280]{1,0:T(8,128)(2,1)S(1)}, f32[640,512]{1,0:T(8,128)S(1)}, f32[512]{0:T(512)S(1)}) custom-call(bf16[192,512]{1,0:T(8,128)(2,1)} %g_hbm.1, bf16[256,1280]{1,0:T(8,128)(2,1)} %x_hbm.1, bf16[5120,512]{1,0:T(8,128)(2,1)} %w_hbm.1, s32[8,8]{1,0:T(8,128)} %it_hbm.1, s32[8]{0:T(128)} %mv_hbm.1), custom_call_target="tpu_custom_call" | custom-call | tf_op jit(solution)/shard_map/pallas_call | solution.py:657
  52.4 1.3 %shard_map.77 = (bf16[256,1280]{1,0:T(8,128)(2,1)}, f32[640,512]{1,0:T(8,128)}, f32[512]{0:T(512)}) custom-call(bf16[256,1280]{1,0:T(8,128)(2,1)S(1)} %get-tuple-element.6.a_ref, f32[640,512]{1,0:T(8,128)S(1)} %get-tuple-element.7.b_ref, f32[512]{0:T(512)S(1)} %get-tuple-element.8.c_ref), custom_call_target="tpu_custom_call" | custom-call | tf_op jit(solution)/shard_map/pallas_call | solution.py:634

commit v6 on v5

--- a/solution.py
+++ b/solution.py
@@ -139,7 +139,6 @@
         greet(dp, z + 1)
         greet(partner, z + 1)
 
-    pl.semaphore_wait(barrier, dpn - 1 + jnp.where(z > 0, 2, 0) + jnp.where(z < n - 1, 2, 0))
 
     def remote(src, dst, ss, rs, d, t):
         return pltpu.make_async_remote_copy(
@@ -148,8 +147,6 @@
 
     x_tail_copy = remote(x_ref.at[slot_rows], xn, xt_s, xt_r, before, z)
     raw_copy = remote(graw.at[core], graw.at[core], core_s, core_r, partner, z)
-    x_copies[0].wait()
-    x_tail_copy.start()
 
     for c in plan_copies:
         c.wait()
@@ -233,8 +230,13 @@
             put(to_other, k, tail_rows, jnp.where(stays(lane), v * own, u * other).astype(BF16))
 
     x_copies[1].wait()
+    gelu_main(late)
+    pl.semaphore_wait(barrier, dpn - 1 + jnp.where(z > 0, 2, 0) + jnp.where(z < n - 1, 2, 0))
+    x_copies[0].wait()
+    x_tail_copy.start()
     for k in early:
-        gelu_main(k)
+        if k > late:
+            gelu_main(k)
         send_first(k, *pieces(k)[0])
     g_copy.wait()
     raw_copy.start()
@@ -548,7 +550,7 @@
         total = total + bias[k]
     bg_ref[...] = total[0]
 
-    for k in range(nk):
+    def keep_tile(k):
         for j in range(2):
             rs = slice(k * lane + j * piece, k * lane + (j + 1) * piece)
             acc = wg_ref[rs, :]
@@ -560,10 +562,16 @@
                 acc = acc + wrecv[role, k, j].astype(F32)
             wg_ref[rs, :] = acc
 
+    for k in range(nk - 2):
+        keep_tile(k)
+
     for k in range(nk):
         last_sum(k + 1)
         at = slice(k * ptile, (k + 1) * ptile)
         xg_ref[0:main, at] = (part[z, k, 0:main, :] * slope[0:main, at]).astype(BF16)
+
+    for k in range(nk - 2, nk):
+        keep_tile(k)
 
     tail_copy.wait_recv()
     xg_ref[tok:rows, :] = trecv[...]

time: 53.9 us -> 53.7 us (level)
  no operation moved by 1% of the time
where the time goes in v6:
time: 53.7 us; the launch traced here: 53.5 us
  Pallas kernels  52.9 us (99%)
  between operations  0.64 us (1%)
    pallas_call x1, Pallas kernels, per_device_fast(): pl.pallas_call(functools.partial(kernel, n, dpn), out_shape=(jax.ShapeDty...  51.6 us
    pallas_call x1, Pallas kernels, write_out(): pl.pallas_call(writer, out_shape=tuple((jax.ShapeDtypeStruct(a.shape, a.d...  1.3 us

profile of v6, /device:TPU:7, one launch (start us, length us, event | category | flops | bytes accessed | tf_op | source)
XLA Modules:
  0.0 53.5 jit_solution(799390233318898155)
XLA Ops:
  0.6 51.6 %shard_map.76 = (bf16[256,1280]{1,0:T(8,128)(2,1)S(1)}, f32[640,512]{1,0:T(8,128)S(1)}, f32[512]{0:T(512)S(1)}) custom-call(bf16[192,512]{1,0:T(8,128)(2,1)} %g_hbm.1, bf16[256,1280]{1,0:T(8,128)(2,1)} %x_hbm.1, bf16[5120,512]{1,0:T(8,128)(2,1)} %w_hbm.1, s32[8,8]{1,0:T(8,128)} %it_hbm.1, s32[8]{0:T(128)} %mv_hbm.1), custom_call_target="tpu_custom_call" | custom-call | tf_op jit(solution)/shard_map/pallas_call | solution.py:665
  52.2 1.3 %shard_map.77 = (bf16[256,1280]{1,0:T(8,128)(2,1)}, f32[640,512]{1,0:T(8,128)}, f32[512]{0:T(512)}) custom-call(bf16[256,1280]{1,0:T(8,128)(2,1)S(1)} %get-tuple-element.6.a_ref, f32[640,512]{1,0:T(8,128)S(1)} %get-tuple-element.7.b_ref, f32[512]{0:T(512)S(1)} %get-tuple-element.8.c_ref), custom_call_target="tpu_custom_call" | custom-call | tf_op jit(solution)/shard_map/pallas_call | solution.py:642
